TPU v7x, 32 devices: a whole 2x2x4 slice. The times are simulated.
32 devices in a mesh: dp: 8 (over z, x), mp: 4 (over y, core).
Axes of the slice: x: 2, y: 2, z: 4, core: 2. Of those that a mesh axis runs over, the one named last changes fastest.
Arguments:
- acts: bfloat16 [2048, 4096], P('dp'), may hold values from -6 to 6
- cotangent: bfloat16 [2048, 2048], P('dp', 'mp'), may hold values from -0.13183594 to 0.13183594
- stats: float32 [4, 8, 2, 512, 512], P('mp', 'dp'), as said below
- owner_slot: int32 [8], replicated, may hold values from 0 to 7, as said below
Outputs:
- update: bfloat16 [8, 512, 2048], P(None, 'dp', 'mp')
- new_stats: float32 [4, 8, 2, 512, 512], P('mp', 'dp')
Inputs may be any that keep to these rules, and one draw needn't show every extreme that they name: Distinct slot numbers; row block w is held by device owner_slot[w] // 1 of dp at its position owner_slot[w] % 1; some device holds 1 block. Every stats[j, s, f] is a symmetric positive definite matrix.
All inputs are finite; a program needn't handle non-finite values.
Results may differ from a plain program's by a relative error of at most 0.012.
The roundings to bfloat16 on the way count: a program that leaves them out, or rounds other values in their place, can miss the bound.
Values may be sent and summed in bfloat16 or wider, within the bound.
A program may use at most 192 MiB of HBM per device.

v0:
```python
import jax
import jax.numpy as jnp
from jax import lax
from jax.sharding import PartitionSpec as P

ITERS = 5
BETA = 0.9
DAMPING = 0.001
EPSILON = 1e-06


def batched(former, latter):
    return jnp.einsum(
        "kij,kjl->kil",
        former.astype(jnp.bfloat16),
        latter.astype(jnp.bfloat16),
        preferred_element_type=jnp.float32,
    )


def inverse_roots(stat_pair):
    identity = jnp.eye(stat_pair.shape[-1], dtype=jnp.float32)
    damped = stat_pair + DAMPING * identity
    frob_norm = jnp.sqrt(jnp.sum(damped * damped, axis=(1, 2), keepdims=True) + EPSILON)
    moment = damped / frob_norm
    result = jnp.broadcast_to(identity, stat_pair.shape)
    for iteration in range(ITERS):
        factor = (5.0 * identity - moment) * 0.25
        if iteration == 0:
            result = factor
        else:
            result = batched(result, factor)
        if iteration + 1 < ITERS:
            square = batched(factor, factor)
            moment = batched(square, batched(square, moment))
    return result * frob_norm ** (-0.25)


def precondition(grad_block, stat_pair):
    gram_left = lax.dot_general(
        grad_block, grad_block, (((1,), (1,)), ((), ())), preferred_element_type=jnp.float32
    )
    gram_right = lax.dot_general(
        grad_block, grad_block, (((0,), (0,)), ((), ())), preferred_element_type=jnp.float32
    )
    new_pair = BETA * stat_pair + (1.0 - BETA) * jnp.stack([gram_left, gram_right])
    root_pair = inverse_roots(new_pair)
    left_applied = jnp.dot(
        root_pair[0].astype(jnp.bfloat16), grad_block, preferred_element_type=jnp.float32
    )
    direction = jnp.dot(
        left_applied.astype(jnp.bfloat16),
        root_pair[1].astype(jnp.bfloat16),
        preferred_element_type=jnp.float32,
    )
    grad_wide = grad_block.astype(jnp.float32)
    graft_ratio = jnp.sqrt(
        (jnp.mean(grad_wide * grad_wide) + EPSILON) / (jnp.mean(direction * direction) + EPSILON)
    )
    return ((direction * graft_ratio).astype(jnp.bfloat16), new_pair)


def keep_slot(grad_block, stat_pair):
    return (jnp.zeros_like(grad_block), stat_pair)


def on_device(acts, cotangent, stats, owner_slot):
    dp_count = lax.axis_size("dp")
    my_index = lax.axis_index("dp")
    blk_size = cotangent.shape[1]
    blocks = acts.shape[1] // blk_size
    slot_count = stats.shape[1]
    piece_rows = blk_size // dp_count
    split_acts = acts.reshape(acts.shape[0], blocks, blk_size)
    my_slots = my_index * slot_count + jnp.arange(slot_count, dtype=jnp.int32)
    holds_block = owner_slot[None, :] == my_slots[:, None]
    filled = jnp.any(holds_block, axis=1)
    my_rows = lax.psum_scatter(
        jnp.einsum("twr,tc->rwc", split_acts, cotangent, preferred_element_type=jnp.float32),
        "dp",
        scatter_dimension=0,
        tiled=True,
    ).astype(jnp.bfloat16)
    slot_ids = jnp.arange(dp_count * slot_count, dtype=jnp.int32)
    selector = (owner_slot[None, :] == slot_ids[:, None]).astype(jnp.bfloat16)
    outgoing = jnp.einsum(
        "sw,rwc->src", selector, my_rows, preferred_element_type=jnp.float32
    ).astype(jnp.bfloat16)
    outgoing = outgoing.reshape(dp_count, slot_count, piece_rows, blk_size)
    arrived = lax.all_to_all(outgoing, "dp", split_axis=0, concat_axis=2, tiled=True)
    owned_grads = arrived.reshape(slot_count, blk_size, blk_size)
    slot_update, slot_stats = lax.cond(
        filled[0], precondition, keep_slot, owned_grads[0], stats[0, 0]
    )
    update_list = [slot_update]
    stat_list = [slot_stats]
    updates = jnp.stack(update_list)
    new_stats = jnp.stack(stat_list)[None]
    outgoing_rows = updates.reshape(slot_count, dp_count, piece_rows, blk_size)
    returned = lax.all_to_all(outgoing_rows, "dp", split_axis=1, concat_axis=1, tiled=True)
    grid_ids = (
        jnp.arange(slot_count, dtype=jnp.int32)[:, None]
        + slot_count * jnp.arange(dp_count, dtype=jnp.int32)[None, :]
    )
    picker = (owner_slot[:, None, None] == grid_ids[None]).astype(jnp.bfloat16)
    result = jnp.einsum(
        "wsn,snrc->wrc", picker, returned, preferred_element_type=jnp.float32
    ).astype(jnp.bfloat16)
    return (result, new_stats)


def solution(mesh):
    return jax.shard_map(
        on_device,
        mesh=mesh,
        in_specs=(P("dp", None), P("dp", "mp"), P("mp", "dp", None, None, None), P()),
        out_specs=(P(None, "dp", "mp"), P("mp", "dp", None, None, None)),
        check_vma=False,
    )
```

profile of v0, /device:TPU:0, one launch (start us, length us, event | category | flops | bytes accessed | tf_op | source)
XLA Modules:
  0.0 265.3 jit_solution(8592918326225802116)
XLA Ops:
  7.2 0.0 copy-start
  7.2 0.0 reduce-scatter.2.cloned.1.call-start
  7.2 0.0 copy-start.8
  7.2 3.2 %copy.27 = f32[1,1,2,512,512]{4,3,2,1,0:T(8,128)} copy(f32[1,1,2,512,512]{4,3,2,1,0:T(8,128)} %param.8) | data formatting | bytes 4194304
  10.5 0.0 copy-done.8
  10.5 0.9 copy.17
  11.4 3.5 %copy.11 = bf16[256,8,512]{0,1,2:T(8,128)(2,1)} copy(bf16[256,8,512]{2,1,0:T(8,128)(2,1)S(1)} %bitcast.62) | data formatting | bytes 4194304 | tf_op jit(solution)/shard_map/reshape | solution.py:74
  14.8 0.0 copy-done
  14.8 6.1 %convolution_bitcast_fusion.2 = f32[512,8,512]{2,1,0:T(8,128)} fusion(bf16[256,8,512]{0,1,2:T(8,128)(2,1)} %copy.11, bf16[256,512]{1,0:T(8,128)(2,1)S(1)} %copy-done), kind=kOutput, calls=%fused_computation.43 | convolution fusion | flops 1073741824 | bytes 10747904 | tf_op jit(solution)/shard_map/twr,tc->rwc/dot_general | solution.py:79
  20.9 0.0 copy-start.9
  20.9 0.0 reduce-scatter.2.cloned.1.call-update
  20.9 150.3 %reduce-scatter.2.cloned.1.call-done = f32[64,8,512]{2,1,0:T(8,128)} async-done(((f32[512,8,512]{2,1,0:T(8,128)}), f32[64,8,512]{2,1,0:T(8,128)}) %reduce-scatter.2.cloned.1.call-update) | async-done | bytes 1048592 | tf_op jit(solution)/shard_map/reduce_scatter | solution.py:78
  171.3 0.0 copy-done.9
  171.3 1.5 fusion.16
  172.8 0.9 copy.12
  173.7 3.7 %all-to-all-start = ((bf16[8,1,64,512]{3,2,1,0:T(8,128)(2,1)}), bf16[8,1,64,512]{3,2,1,0:T(8,128)(2,1)S(1)}, u32[]{:S(2)}, u32[]{:S(2)}) async-start(bf16[8,1,64,512]{3,2,1,0:T(8,128)(2,1)} %copy.12), calls=%async_computation.1 | async-start | bytes 1048576 | tf_op jit(solution)/shard_map/all_to_all | solution.py:90
  177.5 0.7 compare_reduce_fusion
  178.9 13.2 %all-to-all-done = bf16[8,1,64,512]{3,2,1,0:T(8,128)(2,1)S(1)} async-done(((bf16[8,1,64,512]{3,2,1,0:T(8,128)(2,1)}), bf16[8,1,64,512]{3,2,1,0:T(8,128)(2,1)S(1)}, u32[]{:S(2)}, u32[]{:S(2)}) %all-to-all-start) | async-done | bytes 524320 | tf_op jit(solution)/shard_map/all_to_all | solution.py:90
  192.1 46.7 %conditional.1 = (bf16[512,512]{1,0:T(8,128)(2,1)}, f32[2,512,512]{2,1,0:T(8,128)}) conditional(s32[]{:T(128)} %convert_element_type.105, f32[2,512,512]{2,1,0:T(8,128)} %bitcast.65, (f32[2,512,512]{2,1,0:T(8,128)}, bf16[8,1,64,512]{3,2,1,0:T(8,128)(2,1)S(1)}) %tuple.32), branch_computations={%region_2.0_spmd, %region_3.0_spmd} | conditional | flops 9696444416 | bytes 114819456 | solution.py:92
  192.1 0.1 fusion.13
  192.2 0.0 copy-start.7
  192.2 0.5 convolution_bitcast_fusion.1
  192.7 0.2 copy-done.3
  192.9 0.5 convolution_bitcast_fusion
  193.4 1.1 copy-done.5
  194.5 1.6 multiply_reduce_fusion
  196.1 0.0 copy-done.7
  196.1 1.3 copy-done.6
  197.4 2.2 convolution_convert_fusion.10
  199.6 3.8 %fusion.1 = f32[2,512,512]{2,1,0:T(8,128)S(1)} fusion(bf16[2,512,512]{2,1,0:T(8,128)(2,1)} %convolution_convert_fusion.10, f32[2,512,512]{2,1,0:T(8,128)} %copy-done.6, f32[2]{0:T(128)S(1)} %get-tuple-element.29, f32[512,512]{1,0:T(8,128)} %copy-done.7), kind=kOutput, calls=%fused_computation.21 | convolution fusion | flops 1075838976 | bytes 6291464 | tf_op jit(solution)/shard_map/cond/branch_1_fun/kij,kjl->kil/dot_general | solution.py:13
  203.4 0.0 copy-start.2
  203.4 1.3 copy-done.2
  204.8 1.7 convolution_convert_fusion.7
  206.5 3.5 %fusion.2 = f32[2,512,512]{2,1,0:T(8,128)S(1)} fusion(bf16[2,512,512]{2,1,0:T(8,128)(2,1)} %convolution_convert_fusion.7, f32[2,512,512]{2,1,0:T(8,128)} %copy-done.2), kind=kOutput, calls=%fused_computation.22 | convolution fusion | flops 1074790400 | bytes 5242880 | tf_op jit(solution)/shard_map/cond/branch_1_fun/kij,kjl->kil/dot_general | solution.py:13
  210.0 5.0 %convolution_convert_fusion.5 = bf16[2,512,512]{2,1,0:T(8,128)(2,1)} fusion(f32[512,512]{1,0:T(8,128)S(1)} %get-tuple-element.33, f32[2,512,512]{2,1,0:T(8,128)} %copy-done.2, f32[2,512,512]{2,1,0:T(8,128)S(1)} %fusion.2, f32[2,512,512]{2,1,0:T(8,128)} %copy-done.6, f32[2]{0:T(128)S(1)} %get-tuple-element.29, f32[512,512]{1,0:T(8,128)} %copy-done.7), kind=kOutput, calls=%fused_computation.15 | convolution fusion | flops 1080557568 | bytes 9437192 | tf_op jit(solution)/shard_map/cond/branch_1_fun/kij,kjl->kil/dot_general | solution.py:13
  215.0 1.7 convolution_convert_fusion.4
  216.7 4.2 %fusion.3 = f32[2,512,512]{2,1,0:T(8,128)} fusion(bf16[2,512,512]{2,1,0:T(8,128)(2,1)} %convolution_convert_fusion.4, f32[2,512,512]{2,1,0:T(8,128)S(1)} %fusion.2), kind=kOutput, calls=%fused_computation.23 | convolution fusion | flops 1074790400 | bytes 5242880 | tf_op jit(solution)/shard_map/cond/branch_1_fun/kij,kjl->kil/dot_general | solution.py:13
  220.9 4.1 %convolution_convert_fusion.1 = bf16[2,512,512]{2,1,0:T(8,128)(2,1)} fusion(f32[2,512,512]{2,1,0:T(8,128)} %fusion.3, f32[512,512]{1,0:T(8,128)S(1)} %get-tuple-element.33), kind=kOutput, calls=%fused_computation.11 | convolution fusion | flops 538968064 | bytes 4194304 | tf_op jit(solution)/shard_map/cond/branch_1_fun/kij,kjl->kil/dot_general | solution.py:13
  225.0 0.0 copy-done.1
  225.0 3.8 %multiply_convert_fusion.1 = bf16[2,512,512]{2,1,0:T(8,128)(2,1)} fusion(bf16[2,512,512]{2,1,0:T(8,128)(2,1)} %convolution_convert_fusion.1, f32[2,512,512]{2,1,0:T(8,128)S(1)} %copy-done.1, f32[512,512]{1,0:T(8,128)S(1)} %get-tuple-element.33), kind=kOutput, calls=%fused_computation.3 | convolution fusion | flops 1076363264 | bytes 5242880 | tf_op jit(solution)/shard_map/cond/branch_1_fun/kij,kjl->kil/dot_general | solution.py:13
  228.8 3.9 %multiply_convert_fusion = bf16[2,512,512]{2,1,0:T(8,128)(2,1)} fusion(bf16[2,512,512]{2,1,0:T(8,128)(2,1)} %multiply_convert_fusion.1, bf16[2,512,512]{2,1,0:T(8,128)(2,1)} %convolution_convert_fusion.5, f32[2]{0:T(128)S(1)} %get-tuple-element.28, f32[2,512,512]{2,1,0:T(8,128)S(1)} %copy-done.1, f32[512,512]{1,0:T(8,128)S(1)} %get-tuple-element.33), kind=kOutput, calls=%fused_computation.2 | convolution fusion | flops 1076887552 | bytes 6291464 | tf_op jit(solution)/shard_map/cond/branch_1_fun/kij,kjl->kil/dot_general | solution.py:13
  232.6 2.9 %multiply_reduce_fusion.1 = (f32[]{:T(128)}, f32[512,512]{1,0:T(8,128)S(1)}) fusion(bf16[2,512,512]{2,1,0:T(8,128)(2,1)} %multiply_convert_fusion, bf16[512,512]{1,0:T(8,128)(2,1)} %bitcast.64), kind=kOutput, calls=%fused_computation.29 | convolution fusion | flops 537657344 | bytes 2621444 | tf_op jit(solution)/shard_map/cond/branch_1_fun/dot_general | solution.py:51
  236.3 0.0 copy-done.4
  236.3 0.9 multiply_reduce_fusion.2
  237.9 0.9 multiply_convert_fusion.6
  238.8 18.3 %all_to_all.14 = bf16[1,8,64,512]{3,2,0,1:T(8,128)(2,1)S(1)} all-to-all(bf16[1,8,64,512]{3,2,0,1:T(8,128)(2,1)} %bitcast.16), channel_id=1, replica_groups=mesh['dp'=8,'mp'=4] {'dp'}, dimensions={1} | all-to-all | bytes 1048576 | tf_op jit(solution)/shard_map/all_to_all | solution.py:100
  257.1 0.4 convolution_convert_fusion.12
  257.5 0.9 copy.16
  (6 shorter events, 0.0 us)
Async XLA Ops:
  7.2 7.7 %copy-start = (bf16[256,512]{1,0:T(8,128)(2,1)S(1)}, bf16[256,512]{1,0:T(8,128)(2,1)}, u32[]{:S(2)}) copy-start(bf16[256,512]{1,0:T(8,128)(2,1)} %param.7) | copy-start | bytes 786436
  7.2 164.1 %reduce-scatter.2.cloned.1.call-start = ((), (), s32[]{:S(2)}) async-start(), calls=%async_computation.3 | async-start | bytes 9437184 | tf_op jit(solution)/shard_map/reduce_scatter | solution.py:78
  7.2 3.2 %copy-start.8 = (bf16[256,4096]{1,0:T(8,128)(2,1)S(1)}, bf16[256,4096]{1,0:T(8,128)(2,1)}, u32[]{:S(2)}) copy-start(bf16[256,4096]{1,0:T(8,128)(2,1)} %param.6) | copy-start | bytes 6291460
  20.9 150.4 %copy-start.9 = (s32[8]{0:T(128)S(1)}, s32[8]{0:T(128)}, u32[]{:S(2)}) copy-start(s32[8]{0:T(128)} %param.9) | copy-start | bytes 100
  173.7 18.4 %all-to-all-start = ((bf16[8,1,64,512]{3,2,1,0:T(8,128)(2,1)}), bf16[8,1,64,512]{3,2,1,0:T(8,128)(2,1)S(1)}, u32[]{:S(2)}, u32[]{:S(2)}) async-start(bf16[8,1,64,512]{3,2,1,0:T(8,128)(2,1)} %copy.12), calls=%async_computation.1 | async-start | bytes 1048576 | tf_op jit(solution)/shard_map/all_to_all | solution.py:90
  192.1 0.8 copy-start.3
  192.2 3.9 %copy-start.7 = (f32[512,512]{1,0:T(8,128)}, f32[512,512]{1,0:T(8,128)S(1)}, u32[]{:S(2)}) copy-start(f32[512,512]{1,0:T(8,128)S(1)} %get-tuple-element.32) | copy-start | bytes 3145732 | tf_op jit(solution)/shard_map/cond
  192.9 1.6 copy-start.5
  196.1 1.3 copy-start.6
  203.4 1.4 copy-start.2
  220.9 4.1 %copy-start.1 = (f32[2,512,512]{2,1,0:T(8,128)S(1)}, f32[2,512,512]{2,1,0:T(8,128)}, u32[]{:S(2)}) copy-start(f32[2,512,512]{2,1,0:T(8,128)} %fusion.3) | copy-start | bytes 6291460 | tf_op jit(solution)/shard_map/cond
  232.6 3.6 %copy-start.4 = (bf16[8,1,64,512]{3,2,1,0:T(8,128)(2,1)S(1)}, bf16[8,1,64,512]{3,2,1,0:T(8,128)(2,1)}, u32[]{:S(2)}) copy-start(bf16[8,1,64,512]{3,2,1,0:T(8,128)(2,1)} %copy-done.3) | copy-start | bytes 1572868 | tf_op jit(solution)/shard_map/cond
Sparse Core Ops, SparseCore 0:
  21.1 150.1 reduce-scatter.1
where the time goes:
time: 266 us; the launch traced here: 265 us
  waiting for transfers between devices  164 us (62%)
  matrix products  45.7 us (17%)
  blocking collectives  18.3 us (7%)
  between operations  14.8 us (6%)
  local copies, waits for them, and re-layouts  13.5 us (5%)
  other arithmetic  4.26 us (2%)
  starting transfers between devices  3.75 us (1%)
    reduce_scatter x1, waiting for transfers between devices, on_device(): lax.psum_scatter(jnp.einsum('twr,tc->rwc', split_acts, cotangent, preferr...  150 us
    dot_general x10, matrix products, batched(): jnp.einsum('kij,kjl->kil', former.astype(jnp.bfloat16), latter.astype(jnp...  33.9 us
    all_to_all x1, blocking collectives, on_device(): lax.all_to_all(outgoing_rows, 'dp', split_axis=1, concat_axis=1, tiled=True)  18.3 us
    all_to_all x1, waiting for transfers between devices, on_device(): lax.all_to_all(outgoing, 'dp', split_axis=0, concat_axis=2, tiled=True)  13.2 us
    dot_general x1, matrix products, on_device(): jnp.einsum('twr,tc->rwc', split_acts, cotangent, preferred_element_type=j...  6.07 us
  transfers between devices with their start and end apart: 2, of which 2 were waited for; matrix products, arithmetic and copies ran while one was open for 0% of the time, Pallas kernels for 0%

commit v1 on v0

--- a/solution.py
+++ b/solution.py
@@ -87,7 +87,10 @@
         "sw,rwc->src", selector, my_rows, preferred_element_type=jnp.float32
     ).astype(jnp.bfloat16)
     outgoing = outgoing.reshape(dp_count, slot_count, piece_rows, blk_size)
-    arrived = lax.all_to_all(outgoing, "dp", split_axis=0, concat_axis=2, tiled=True)
+    arrived = jnp.concatenate(
+        lax.all_to_all(jnp.stack(jnp.split(outgoing, lax.axis_size("dp"), axis=0)), "dp", 0, 0),
+        axis=2,
+    )
     owned_grads = arrived.reshape(slot_count, blk_size, blk_size)
     slot_update, slot_stats = lax.cond(
         filled[0], precondition, keep_slot, owned_grads[0], stats[0, 0]

time: 266 us -> 271 us (1.019)
  local copies, waits for them, and re-layouts: 13.5 us -> 18.6 us
    unnamed x9 -> x16, local copies, waits for them, and re-layouts: 5.09 us -> 9.57 us
where the time goes in v1:
time: 271 us; the launch traced here: 270 us
  waiting for transfers between devices  164 us (61%)
  matrix products  45.6 us (17%)
  local copies, waits for them, and re-layouts  18.6 us (7%)
  blocking collectives  18.3 us (7%)
  between operations  14.6 us (5%)
  other arithmetic  4.17 us (2%)
  starting transfers between devices  3.76 us (1%)
    reduce_scatter x1, waiting for transfers between devices, on_device(): lax.psum_scatter(jnp.einsum('twr,tc->rwc', split_acts, cotangent, preferr...  150 us
    dot_general x10, matrix products, batched(): jnp.einsum('kij,kjl->kil', former.astype(jnp.bfloat16), latter.astype(jnp...  33.8 us
    all_to_all x1, blocking collectives, on_device(): lax.all_to_all(outgoing_rows, 'dp', split_axis=1, concat_axis=1, tiled=True)  18.3 us
    all_to_all x1, waiting for transfers between devices, on_device(): lax.all_to_all(jnp.stack(jnp.split(outgoing, lax.axis_size('dp'), axis=0)...  13.4 us
    unnamed x16, local copies, waits for them, and re-layouts  9.57 us
    dot_general x1, matrix products, on_device(): jnp.einsum('twr,tc->rwc', split_acts, cotangent, preferred_element_type=j...  6.08 us
  transfers between devices with their start and end apart: 2, of which 2 were waited for; matrix products, arithmetic and copies ran while one was open for 0% of the time, Pallas kernels for 0%

profile of v1, /device:TPU:0, one launch (start us, length us, event | category | flops | bytes accessed | tf_op | source)
XLA Modules:
  0.0 270.2 jit_solution(17714748441440273184)
XLA Ops:
  7.2 0.0 copy-start
  7.2 0.0 reduce-scatter.2.cloned.1.call-start
  7.2 3.2 %copy.105 = f32[1,1,2,512,512]{4,3,2,1,0:T(8,128)} copy(f32[1,1,2,512,512]{4,3,2,1,0:T(8,128)} %param.8) | data formatting | bytes 4194304
  10.5 0.9 copy.80
  11.4 3.5 %copy.67 = bf16[256,8,512]{0,1,2:T(8,128)(2,1)} copy(bf16[256,8,512]{2,1,0:T(8,128)(2,1)S(1)} %bitcast.77) | data formatting | bytes 4194304 | tf_op jit(solution)/shard_map/reshape | solution.py:74
  14.8 0.0 copy-done
  14.8 6.1 %convolution_bitcast_fusion.2 = f32[512,8,512]{2,1,0:T(8,128)} fusion(bf16[256,8,512]{0,1,2:T(8,128)(2,1)} %copy.67, bf16[256,512]{1,0:T(8,128)(2,1)S(1)} %copy-done), kind=kOutput, calls=%fused_computation.43 | convolution fusion | flops 1073741824 | bytes 10747904 | tf_op jit(solution)/shard_map/twr,tc->rwc/dot_general | solution.py:79
  20.9 0.0 reduce-scatter.2.cloned.1.call-update
  20.9 150.3 %reduce-scatter.2.cloned.1.call-done = f32[64,8,512]{2,1,0:T(8,128)} async-done(((f32[512,8,512]{2,1,0:T(8,128)}), f32[64,8,512]{2,1,0:T(8,128)}) %reduce-scatter.2.cloned.1.call-update) | async-done | bytes 1048592 | tf_op jit(solution)/shard_map/reduce_scatter | solution.py:78
  171.3 1.5 convolution_convert_fusion.13
  172.8 0.9 fusion.27
  173.7 0.6 bitcast_dynamic-update-slice_fusion.7
  174.4 0.6 bitcast_dynamic-update-slice_fusion.6
  175.0 0.6 bitcast_dynamic-update-slice_fusion.5
  175.7 0.6 bitcast_dynamic-update-slice_fusion.4
  176.3 0.6 bitcast_dynamic-update-slice_fusion.3
  176.9 0.6 bitcast_dynamic-update-slice_fusion.2
  177.6 0.6 bitcast_dynamic-update-slice_fusion.1
  178.2 0.6 bitcast_dynamic-update-slice_fusion
  178.9 3.7 %all-to-all-start = ((bf16[8,1,1,64,512]{4,3,2,1,0:T(8,128)(2,1)}), bf16[8,1,1,64,512]{4,3,2,1,0:T(8,128)(2,1)S(1)}, u32[]{:S(2)}, u32[]{:S(2)}) async-start(bf16[8,1,1,64,512]{4,3,2,1,0:T(8,128)(2,1)} %bitcast_dynamic-update-slice_fusion), calls=%async_computation.1 | async-start | bytes 1048576 | tf_op jit(solution)/shard_map/all_to_all | solution.py:91
  182.6 0.6 compare_reduce_fusion
  183.8 13.4 %all-to-all-done = bf16[8,1,1,64,512]{4,3,2,1,0:T(8,128)(2,1)S(1)} async-done(((bf16[8,1,1,64,512]{4,3,2,1,0:T(8,128)(2,1)}), bf16[8,1,1,64,512]{4,3,2,1,0:T(8,128)(2,1)S(1)}, u32[]{:S(2)}, u32[]{:S(2)}) %all-to-all-start) | async-done | bytes 524320 | tf_op jit(solution)/shard_map/all_to_all | solution.py:91
  197.2 46.4 %conditional.1 = (bf16[512,512]{1,0:T(8,128)(2,1)}, f32[2,512,512]{2,1,0:T(8,128)}) conditional(s32[]{:T(128)} %convert_element_type.105, f32[2,512,512]{2,1,0:T(8,128)} %bitcast.80, (f32[2,512,512]{2,1,0:T(8,128)}, bf16[8,1,1,64,512]{4,3,2,1,0:T(8,128)(2,1)S(1)}) %tuple.53), branch_computations={%region_2.0_spmd, %region_3.0_spmd} | conditional | flops 9696444416 | bytes 114819456 | solution.py:95
  197.2 0.1 fusion.13
  197.4 0.0 copy-start.7
  197.4 0.5 convolution_bitcast_fusion.1
  197.8 0.2 copy-done.3
  198.0 0.5 convolution_bitcast_fusion
  198.5 1.1 copy-done.5
  199.6 1.6 multiply_reduce_fusion
  201.3 1.3 copy-done.6
  202.5 2.2 convolution_convert_fusion.10
  204.7 3.8 %fusion.1 = f32[2,512,512]{2,1,0:T(8,128)S(1)} fusion(bf16[2,512,512]{2,1,0:T(8,128)(2,1)} %convolution_convert_fusion.10, f32[2,512,512]{2,1,0:T(8,128)} %copy-done.6, f32[2]{0:T(128)S(1)} %get-tuple-element.57, f32[512,512]{1,0:T(8,128)} %copy-done.7), kind=kOutput, calls=%fused_computation.21 | convolution fusion | flops 1075838976 | bytes 6291464 | tf_op jit(solution)/shard_map/cond/branch_1_fun/kij,kjl->kil/dot_general | solution.py:13
  208.6 1.3 copy-done.2
  209.9 1.7 convolution_convert_fusion.7
  211.6 3.5 %fusion.2 = f32[2,512,512]{2,1,0:T(8,128)S(1)} fusion(bf16[2,512,512]{2,1,0:T(8,128)(2,1)} %convolution_convert_fusion.7, f32[2,512,512]{2,1,0:T(8,128)} %copy-done.2), kind=kOutput, calls=%fused_computation.22 | convolution fusion | flops 1074790400 | bytes 5242880 | tf_op jit(solution)/shard_map/cond/branch_1_fun/kij,kjl->kil/dot_general | solution.py:13
  215.1 5.0 %convolution_convert_fusion.5 = bf16[2,512,512]{2,1,0:T(8,128)(2,1)} fusion(f32[512,512]{1,0:T(8,128)S(1)} %get-tuple-element.61, f32[2,512,512]{2,1,0:T(8,128)} %copy-done.2, f32[2,512,512]{2,1,0:T(8,128)S(1)} %fusion.2, f32[2,512,512]{2,1,0:T(8,128)} %copy-done.6, f32[2]{0:T(128)S(1)} %get-tuple-element.57, f32[512,512]{1,0:T(8,128)} %copy-done.7), kind=kOutput, calls=%fused_computation.15 | convolution fusion | flops 1080557568 | bytes 9437192 | tf_op jit(solution)/shard_map/cond/branch_1_fun/kij,kjl->kil/dot_general | solution.py:13
  220.1 1.7 convolution_convert_fusion.4
  221.8 4.1 %fusion.3 = f32[2,512,512]{2,1,0:T(8,128)} fusion(bf16[2,512,512]{2,1,0:T(8,128)(2,1)} %convolution_convert_fusion.4, f32[2,512,512]{2,1,0:T(8,128)S(1)} %fusion.2), kind=kOutput, calls=%fused_computation.23 | convolution fusion | flops 1074790400 | bytes 5242880 | tf_op jit(solution)/shard_map/cond/branch_1_fun/kij,kjl->kil/dot_general | solution.py:13
  226.0 4.1 %convolution_convert_fusion.1 = bf16[2,512,512]{2,1,0:T(8,128)(2,1)} fusion(f32[2,512,512]{2,1,0:T(8,128)} %fusion.3, f32[512,512]{1,0:T(8,128)S(1)} %get-tuple-element.61), kind=kOutput, calls=%fused_computation.11 | convolution fusion | flops 538968064 | bytes 4194304 | tf_op jit(solution)/shard_map/cond/branch_1_fun/kij,kjl->kil/dot_general | solution.py:13
  230.1 3.8 %multiply_convert_fusion.1 = bf16[2,512,512]{2,1,0:T(8,128)(2,1)} fusion(bf16[2,512,512]{2,1,0:T(8,128)(2,1)} %convolution_convert_fusion.1, f32[2,512,512]{2,1,0:T(8,128)S(1)} %copy-done.1, f32[512,512]{1,0:T(8,128)S(1)} %get-tuple-element.61), kind=kOutput, calls=%fused_computation.3 | convolution fusion | flops 1076363264 | bytes 5242880 | tf_op jit(solution)/shard_map/cond/branch_1_fun/kij,kjl->kil/dot_general | solution.py:13
  233.8 3.9 %multiply_convert_fusion = bf16[2,512,512]{2,1,0:T(8,128)(2,1)} fusion(bf16[2,512,512]{2,1,0:T(8,128)(2,1)} %multiply_convert_fusion.1, bf16[2,512,512]{2,1,0:T(8,128)(2,1)} %convolution_convert_fusion.5, f32[2]{0:T(128)S(1)} %get-tuple-element.56, f32[2,512,512]{2,1,0:T(8,128)S(1)} %copy-done.1, f32[512,512]{1,0:T(8,128)S(1)} %get-tuple-element.61), kind=kOutput, calls=%fused_computation.2 | convolution fusion | flops 1076887552 | bytes 6291464 | tf_op jit(solution)/shard_map/cond/branch_1_fun/kij,kjl->kil/dot_general | solution.py:13
  237.7 2.9 %multiply_reduce_fusion.1 = (f32[]{:T(128)}, f32[512,512]{1,0:T(8,128)S(1)}) fusion(bf16[2,512,512]{2,1,0:T(8,128)(2,1)} %multiply_convert_fusion, bf16[512,512]{1,0:T(8,128)(2,1)} %bitcast.79), kind=kOutput, calls=%fused_computation.29 | convolution fusion | flops 537657344 | bytes 2621444 | tf_op jit(solution)/shard_map/cond/branch_1_fun/dot_general | solution.py:51
  241.1 0.9 multiply_reduce_fusion.2
  242.7 0.9 multiply_convert_fusion.6
  243.6 18.3 %all_to_all.10 = bf16[1,8,64,512]{3,2,0,1:T(8,128)(2,1)S(1)} all-to-all(bf16[1,8,64,512]{3,2,0,1:T(8,128)(2,1)} %bitcast.15), channel_id=1, replica_groups=mesh['dp'=8,'mp'=4] {'dp'}, dimensions={1} | all-to-all | bytes 1048576 | tf_op jit(solution)/shard_map/all_to_all | solution.py:103
  261.9 0.4 convolution_convert_fusion.12
  262.4 0.9 copy.71
  (14 shorter events, 0.0 us)
Async XLA Ops:
  7.2 7.7 %copy-start = (bf16[256,512]{1,0:T(8,128)(2,1)S(1)}, bf16[256,512]{1,0:T(8,128)(2,1)}, u32[]{:S(2)}) copy-start(bf16[256,512]{1,0:T(8,128)(2,1)} %param.7) | copy-start | bytes 786436
  7.2 164.1 %reduce-scatter.2.cloned.1.call-start = ((), (), s32[]{:S(2)}) async-start(), calls=%async_computation.3 | async-start | bytes 9437184 | tf_op jit(solution)/shard_map/reduce_scatter | solution.py:78
  7.2 3.2 %copy-start.8 = (bf16[256,4096]{1,0:T(8,128)(2,1)S(1)}, bf16[256,4096]{1,0:T(8,128)(2,1)}, u32[]{:S(2)}) copy-start(bf16[256,4096]{1,0:T(8,128)(2,1)} %param.6) | copy-start | bytes 6291460
  20.9 150.4 %copy-start.9 = (s32[8]{0:T(128)S(1)}, s32[8]{0:T(128)}, u32[]{:S(2)}) copy-start(s32[8]{0:T(128)} %param.9) | copy-start | bytes 100
  178.9 18.3 %all-to-all-start = ((bf16[8,1,1,64,512]{4,3,2,1,0:T(8,128)(2,1)}), bf16[8,1,1,64,512]{4,3,2,1,0:T(8,128)(2,1)S(1)}, u32[]{:S(2)}, u32[]{:S(2)}) async-start(bf16[8,1,1,64,512]{4,3,2,1,0:T(8,128)(2,1)} %bitcast_dynamic-update-slice_fusion), calls=%async_computation.1 | async-start | bytes 1048576 | tf_op jit(solution)/shard_map/all_to_all | solution.py:91
  197.2 0.8 copy-start.3
  197.4 3.9 %copy-start.7 = (f32[512,512]{1,0:T(8,128)}, f32[512,512]{1,0:T(8,128)S(1)}, u32[]{:S(2)}) copy-start(f32[512,512]{1,0:T(8,128)S(1)} %get-tuple-element.60) | copy-start | bytes 3145732 | tf_op jit(solution)/shard_map/cond
  198.0 1.6 copy-start.5
  201.2 1.3 copy-start.6
  208.5 1.3 copy-start.2
  226.0 4.1 %copy-start.1 = (f32[2,512,512]{2,1,0:T(8,128)S(1)}, f32[2,512,512]{2,1,0:T(8,128)}, u32[]{:S(2)}) copy-start(f32[2,512,512]{2,1,0:T(8,128)} %fusion.3) | copy-start | bytes 6291460 | tf_op jit(solution)/shard_map/cond
  237.7 3.4 %copy-start.4 = (bf16[8,1,1,64,512]{4,3,2,1,0:T(8,128)(2,1)S(1)}, bf16[8,1,1,64,512]{4,3,2,1,0:T(8,128)(2,1)}, u32[]{:S(2)}) copy-start(bf16[8,1,1,64,512]{4,3,2,1,0:T(8,128)(2,1)} %copy-done.3) | copy-start | bytes 1572868 | tf_op jit(solution)/shard_map/cond
Sparse Core Ops, SparseCore 0:
  21.1 150.1 reduce-scatter.1
